TPU v7x, 32 devices: a whole 2x2x4 slice. The times are simulated.
32 devices in a mesh: dp: 16 (over z, y, x), mp: 2 (over core).
Axes of the slice: x: 2, y: 2, z: 4, core: 2. Of those that a mesh axis runs over, the one named last changes fastest.
Arguments:
- grad: bfloat16 [4, 1024, 8192], P(None, 'dp', 'mp'), may hold values from -6 to 6
- second_moment: float32 [4, 1024, 8192], P(None, 'dp', 'mp'), may hold values from 0.004 to 20, as said below
- left_root: bfloat16 [2, 16, 1024, 1024], P('mp', 'dp'), as said below
- right_root: bfloat16 [2, 16, 1024, 1024], P('mp', 'dp'), as said below
- owner_slot: int32 [2, 4, 4], replicated, may hold values from 0 to 15, as said below
Outputs:
- update: bfloat16 [4, 1024, 8192], P(None, 'dp', 'mp')
Inputs may be any that keep to these rules, and one draw needn't show every extreme that they name: For each h, owner_slot[h] lists every dp index exactly once: each dp index owns one block of each h. `second_moment`: positive. `left_root`: each square is symmetric positive definite. `right_root`: each square is symmetric positive definite.
All inputs are finite; a program needn't handle non-finite values.
Results may differ from a plain program's by a relative error of at most 0.0049.
Values may be sent and summed in bfloat16 or wider, within the bound.
A program may use at most 64 MiB of HBM per device.

v0:
```python
import jax
import jax.numpy as jnp
from jax import lax
from jax.sharding import PartitionSpec as P

BETA_TWO = 0.99
ADAM_EPS = 1e-08
NORM_EPS = 1e-06


def per_device(grad, second_moment, left_root, right_root, owner_slot):
    row_blocks, block_rows, half_cols = grad.shape
    block_size = left_root.shape[-1]
    col_blocks = half_cols // block_size
    dp_count = lax.axis_size("dp")
    mp_index = lax.axis_index("mp")
    widened = grad.astype(jnp.float32)
    moment_new = BETA_TWO * second_moment + (1.0 - BETA_TWO) * widened * widened
    direction = widened / (jnp.sqrt(moment_new) + ADAM_EPS)
    partial_value = jnp.sum(
        (direction * direction).reshape(row_blocks, block_rows, col_blocks, block_size), axis=(1, 3)
    )
    table = lax.dynamic_index_in_dim(owner_slot, mp_index, 0, keepdims=False)
    owner_ids = lax.iota(jnp.int32, dp_count)
    matches = table[None, :, :] == owner_ids[:, None, None]
    select_half = matches.astype(jnp.bfloat16)
    select_full = matches.astype(jnp.float32).reshape(dp_count, row_blocks * col_blocks)
    tiles = grad.reshape(row_blocks, block_rows, col_blocks, block_size)
    outgoing = jnp.einsum("src,rwck->swk", select_half, tiles, preferred_element_type=jnp.float32)
    outgoing = outgoing.astype(jnp.bfloat16).reshape(dp_count, 1, block_rows, block_size)
    per_owner = jnp.dot(select_full, partial_value.reshape(-1), precision=lax.Precision.HIGHEST)
    arrived_sq = lax.all_to_all(per_owner, "dp", split_axis=0, concat_axis=0, tiled=True)
    adam_sq = jnp.sum(arrived_sq)
    left = left_root[0, 0]
    right = right_root[0, 0]
    arrived = lax.all_to_all(outgoing, "dp", split_axis=0, concat_axis=1, tiled=True)
    block = arrived.reshape(block_size, block_size)
    mixed = jnp.dot(block, right, preferred_element_type=jnp.float32).astype(jnp.bfloat16)
    shaped = jnp.dot(left, mixed, preferred_element_type=jnp.float32)
    shaped_sq = jnp.sum(shaped * shaped)
    factor = jnp.sqrt((adam_sq + NORM_EPS) / (shaped_sq + NORM_EPS))
    result = (shaped * factor).astype(jnp.bfloat16).reshape(1, dp_count, block_rows, block_size)
    back = lax.all_to_all(result, "dp", split_axis=1, concat_axis=0, tiled=True)
    placed = jnp.einsum(
        "src,swk->rwck",
        select_half,
        back.reshape(dp_count, block_rows, block_size),
        preferred_element_type=jnp.float32,
    )
    return placed.astype(jnp.bfloat16).reshape(row_blocks, block_rows, half_cols)


def solution(mesh):
    in_specs = (
        P(None, "dp", "mp"),
        P(None, "dp", "mp"),
        P("mp", "dp", None, None),
        P("mp", "dp", None, None),
        P(),
    )
    out_specs = P(None, "dp", "mp")
    return jax.shard_map(
        per_device, mesh=mesh, in_specs=in_specs, out_specs=out_specs, check_vma=False
    )
```

profile of v0, /device:TPU:0, one launch (start us, length us, event | category | flops | bytes accessed | tf_op | source)
XLA Modules:
  0.0 157.1 jit_solution(964478429440768154)
XLA Ops:
  0.0 0.0 copy-start
  0.0 0.0 copy-start.1
  0.0 5.4 %fusion.4 = f32[4,4096]{1,0:T(4,128)S(1)} fusion(f32[4,64,4096]{2,1,0:T(8,128)} %param.6, bf16[4,64,4096]{2,1,0:T(8,128)(2,1)} %param.5), kind=kLoop, calls=%fused_computation.9 | loop fusion | flops 9420800 | bytes 6356992 | tf_op jit(solution)/shard_map/reduce_sum | solution.py:20
  5.4 0.1 reduce_sum.35
  5.5 0.0 copy-done.1
  5.5 0.1 reduce_sum.36
  5.6 0.9 fusion.21
  6.5 8.3 %all-to-all-start.1 = ((f32[16,1,1]{2,1,0:T(1,128)}), f32[16,1,1]{2,1,0:T(1,128)S(1)}, u32[]{:S(2)}, u32[]{:S(2)}) async-start(f32[16,1,1]{2,1,0:T(1,128)} %bitcast.24), calls=%async_computation.1 | async-start | bytes 16384 | tf_op jit(solution)/shard_map/all_to_all | solution.py:32
  14.9 4.5 %reshape.32 = bf16[4,64,4,1024]{3,2,1,0:T(4,128)(2,1)} reshape(bf16[4,64,4096]{2,1,0:T(8,128)(2,1)} %param.5) | data formatting | bytes 4194304 | tf_op jit(solution)/shard_map/reshape | solution.py:28
  19.4 3.2 %fusion.15 = bf16[16,1,64,1024]{3,0,2,1:T(8,128)(2,1)S(1)} fusion(bf16[4,64,4,1024]{3,2,1,0:T(4,128)(2,1)} %reshape.32, s32[4,4]{1,0:T(4,128)S(1)} %dynamic-slice_bitcast_fusion), kind=kOutput, calls=%fused_computation.19 | convolution fusion | flops 34603264 | bytes 4194368 | tf_op jit(solution)/shard_map/src,rwck->swk/dot_general | solution.py:29
  22.6 2.5 %copy.22 = bf16[16,1,64,1024]{3,2,1,0:T(8,128)(2,1)} copy(bf16[16,1,64,1024]{3,0,2,1:T(8,128)(2,1)S(1)} %fusion.15) | data formatting | bytes 4194304 | tf_op jit(solution)/shard_map/reshape | solution.py:30
  25.1 0.0 all-to-all-done.1
  25.1 7.0 %all-to-all-start = ((bf16[16,1,64,1024]{3,2,1,0:T(8,128)(2,1)}), bf16[16,1,64,1024]{3,2,1,0:T(8,128)(2,1)}, u32[]{:S(2)}, u32[]{:S(2)}) async-start(bf16[16,1,64,1024]{3,2,1,0:T(8,128)(2,1)} %copy.22), calls=%async_computation | async-start | bytes 4194304 | tf_op jit(solution)/shard_map/all_to_all | solution.py:36
  32.0 0.7 reduce_sum.37
  33.4 41.4 %all-to-all-done = bf16[16,1,64,1024]{3,2,1,0:T(8,128)(2,1)} async-done(((bf16[16,1,64,1024]{3,2,1,0:T(8,128)(2,1)}), bf16[16,1,64,1024]{3,2,1,0:T(8,128)(2,1)}, u32[]{:S(2)}, u32[]{:S(2)}) %all-to-all-start) | async-done | bytes 2097184 | tf_op jit(solution)/shard_map/all_to_all | solution.py:36
  74.8 0.0 copy-done
  74.8 9.2 %multiply_reduce_fusion = (f32[]{:T(128)}, f32[1024,1024]{0,1:T(8,128)}) fusion(bf16[1024,1024]{1,0:T(8,128)(2,1)} %bitcast.5, bf16[1,1,1024,1024]{3,2,1,0:T(8,128)(2,1)S(1)} %copy-done, bf16[1,1,1024,1024]{3,2,1,0:T(8,128)(2,1)} %param.7), kind=kOutput, calls=%fused_computation.8 | convolution fusion | flops 4298113024 | bytes 10485764 | tf_op jit(solution)/shard_map/dot_general | solution.py:39
  84.8 2.8 %multiply_convert_fusion = bf16[1024,1024]{0,1:T(8,128)(2,1)S(1)} fusion(f32[1024,1024]{0,1:T(8,128)} %get-tuple-element.6, f32[]{:T(128)S(6)} %sqrt.7), kind=kLoop, calls=%fused_computation.7 | loop fusion | flops 2097152 | bytes 6291460 | tf_op jit(solution)/shard_map/convert_element_type | solution.py:42
  87.6 57.9 %all_to_all.27 = bf16[1,16,64,1024]{3,2,0,1:T(8,128)(2,1)S(1)} all-to-all(bf16[1,16,64,1024]{3,2,0,1:T(8,128)(2,1)S(1)} %bitcast.60), channel_id=1, replica_groups=mesh['dp'=16,'mp'=2] {'dp'}, dimensions={1} | all-to-all | bytes 4194304 | tf_op jit(solution)/shard_map/all_to_all | solution.py:43
  145.4 3.1 %convert_bitcast_fusion = bf16[4,64,4,1024]{3,2,0,1:T(4,128)(2,1)} fusion(bf16[1,16,64,1024]{3,2,0,1:T(8,128)(2,1)S(1)} %all_to_all.27, s32[4,4]{1,0:T(4,128)S(1)} %dynamic-slice_bitcast_fusion), kind=kOutput, calls=%fused_computation.17 | convolution fusion | flops 34603264 | bytes 4194368 | tf_op jit(solution)/shard_map/src,swk->rwck/dot_general | solution.py:44
  148.5 4.5 %reshape.37 = bf16[4,64,4096]{2,0,1:T(4,128)(2,1)} reshape(bf16[4,64,4,1024]{3,2,0,1:T(4,128)(2,1)} %convert_bitcast_fusion) | data formatting | bytes 4194304 | tf_op jit(solution)/shard_map/reshape | solution.py:50
  153.0 4.1 %copy.26 = bf16[4,64,4096]{2,1,0:T(8,128)(2,1)} copy(bf16[4,64,4096]{2,0,1:T(4,128)(2,1)} %reshape.37) | data formatting | bytes 4194304 | tf_op jit(solution)/shard_map/reshape | solution.py:50
  (1 shorter events, 0.0 us)
Async XLA Ops:
  0.0 74.8 %copy-start = (bf16[1,1,1024,1024]{3,2,1,0:T(8,128)(2,1)S(1)}, bf16[1,1,1024,1024]{3,2,1,0:T(8,128)(2,1)}, u32[]{:S(2)}) copy-start(bf16[1,1,1024,1024]{3,2,1,0:T(8,128)(2,1)} %param.8) | copy-start | bytes 6291460
  0.0 5.5 %copy-start.1 = (s32[2,4,4]{2,1,0:T(4,128)S(1)}, s32[2,4,4]{2,1,0:T(4,128)}, u32[]{:S(2)}) copy-start(s32[2,4,4]{2,1,0:T(4,128)} %param.9) | copy-start | bytes 388
  6.5 18.6 %all-to-all-start.1 = ((f32[16,1,1]{2,1,0:T(1,128)}), f32[16,1,1]{2,1,0:T(1,128)S(1)}, u32[]{:S(2)}, u32[]{:S(2)}) async-start(f32[16,1,1]{2,1,0:T(1,128)} %bitcast.24), calls=%async_computation.1 | async-start | bytes 16384 | tf_op jit(solution)/shard_map/all_to_all | solution.py:32
  25.1 49.7 %all-to-all-start = ((bf16[16,1,64,1024]{3,2,1,0:T(8,128)(2,1)}), bf16[16,1,64,1024]{3,2,1,0:T(8,128)(2,1)}, u32[]{:S(2)}, u32[]{:S(2)}) async-start(bf16[16,1,64,1024]{3,2,1,0:T(8,128)(2,1)} %copy.22), calls=%async_computation | async-start | bytes 4194304 | tf_op jit(solution)/shard_map/all_to_all | solution.py:36
where the time goes:
time: 158 us; the launch traced here: 157 us
  blocking collectives  57.9 us (37%)
  waiting for transfers between devices  41.4 us (26%)
  matrix products  16.5 us (10%)
  local copies, waits for them, and re-layouts  15.6 us (10%)
  starting transfers between devices  15.3 us (10%)
  other arithmetic  8.99 us (6%)
    all_to_all x1, blocking collectives, per_device(): back = lax.all_to_all(result, 'dp', split_axis=1, concat_axis=0, tiled=True)  57.9 us
    all_to_all x1, waiting for transfers between devices, per_device(): lax.all_to_all(outgoing, 'dp', split_axis=0, concat_axis=1, tiled=True)  41.4 us
    dot_general x1, matrix products, per_device(): shaped = jnp.dot(left, mixed, preferred_element_type=jnp.float32)  9.24 us
    reshape x2, local copies, waits for them, and re-layouts, per_device(): placed.astype(jnp.bfloat16).reshape(row_blocks, block_rows, half_cols)  8.57 us
    all_to_all x1, starting transfers between devices, per_device(): lax.all_to_all(per_owner, 'dp', split_axis=0, concat_axis=0, tiled=True)  8.34 us
    all_to_all x1, starting transfers between devices, per_device(): lax.all_to_all(outgoing, 'dp', split_axis=0, concat_axis=1, tiled=True)  6.96 us
    reduce_sum x2, other arithmetic, per_device(): jnp.sum((direction * direction).reshape(row_blocks, block_rows, col_block...  5.52 us
    reshape x1, local copies, waits for them, and re-layouts, per_device(): tiles = grad.reshape(row_blocks, block_rows, col_blocks, block_size)  4.49 us
  transfers between devices with their start and end apart: 2, of which 1 were waited for; matrix products, arithmetic and copies ran while one was open for 7% of the time, Pallas kernels for 0%

commit v1 on v0

--- a/solution.py
+++ b/solution.py
@@ -6,6 +6,17 @@
 BETA_TWO = 0.99
 ADAM_EPS = 1e-08
 NORM_EPS = 1e-06
+
+
+def split_up(x, dim, size):
+    before, after = (x.shape[:dim], x.shape[dim + 1 :])
+    return jnp.moveaxis(x.reshape(*before, size, -1, *after), dim, 0)
+
+
+def laid_out(parts, dim):
+    shape = list(parts.shape[1:])
+    shape[dim] *= parts.shape[0]
+    return jnp.moveaxis(parts, 0, dim).reshape(shape)
 
 
 def per_device(grad, second_moment, left_root, right_root, owner_slot):
@@ -33,7 +44,14 @@
     adam_sq = jnp.sum(arrived_sq)
     left = left_root[0, 0]
     right = right_root[0, 0]
-    arrived = lax.all_to_all(outgoing, "dp", split_axis=0, concat_axis=1, tiled=True)
+    size, place = (lax.axis_size("dp"), lax.axis_index("dp"))
+    blocks = split_up(outgoing, 0, size)
+    outs = [blocks[place]]
+    for step in range(1, size):
+        sent = blocks[place ^ step]
+        outs.append(lax.ppermute(sent, "dp", [(i, i ^ step) for i in range(size)]))
+    blocks = jnp.stack(outs)[place ^ jnp.arange(size)]
+    arrived = laid_out(blocks, 1)
     block = arrived.reshape(block_size, block_size)
     mixed = jnp.dot(block, right, preferred_element_type=jnp.float32).astype(jnp.bfloat16)
     shaped = jnp.dot(left, mixed, preferred_element_type=jnp.float32)

time: 158 us -> 181 us (1.15)
  waiting for transfers between devices: 41.4 us -> 7.92 us
  local copies, waits for them, and re-layouts: 15.6 us -> 45.5 us
  starting transfers between devices: 15.3 us -> 41.1 us
    all_to_all x1 -> x0, waiting for transfers between devices: 41.4 us -> none  [per_device(): lax.all_to_all(outgoing, 'dp', split_axis=0, concat_axis=1, tiled=True)]
    ppermute x0 -> x15, starting transfers between devices: none -> 32.7 us  [per_device(): outs.append(lax.ppermute(sent, 'dp', [(i, i ^ step) for i in range(size)]))]
    unnamed x4 -> x34, local copies, waits for them, and re-layouts: 0.01 us -> 17.8 us
    dynamic_slice x0 -> x1, local copies, waits for them, and re-layouts: none -> 10.4 us  [per_device(): sent = blocks[place ^ step]]
    ppermute x0 -> x15, waiting for transfers between devices: none -> 7.91 us  [per_device(): outs.append(lax.ppermute(sent, 'dp', [(i, i ^ step) for i in range(size)]))]
    all_to_all x1 -> x0, starting transfers between devices: 6.96 us -> none  [per_device(): lax.all_to_all(outgoing, 'dp', split_axis=0, concat_axis=1, tiled=True)]
    gather x0 -> x1, local copies, waits for them, and re-layouts: none -> 3.59 us  [per_device(): blocks = jnp.stack(outs)[place ^ jnp.arange(size)]]
    reshape x1 -> x0, local copies, waits for them, and re-layouts: 2.47 us -> none  [per_device(): outgoing.astype(jnp.bfloat16).reshape(dp_count, 1, block_rows, block_size)]
  transfers between devices with their start and end apart: 2 -> 16, of which waited for: 1 -> 2; matrix products, arithmetic and copies ran while one was open for 7% -> 21% of each run, Pallas kernels for 0% -> 0%
where the time goes in v1:
time: 181 us
  blocking collectives  57.9 us (32%)
  local copies, waits for them, and re-layouts  45.5 us (25%)
  starting transfers between devices  41.1 us (23%)
  matrix products  17.8 us (10%)
  other arithmetic  8.99 us (5%)
  waiting for transfers between devices  7.92 us (4%)
    all_to_all x1, blocking collectives, per_device(): back = lax.all_to_all(result, 'dp', split_axis=1, concat_axis=0, tiled=True)  57.9 us
    ppermute x15, starting transfers between devices, per_device(): outs.append(lax.ppermute(sent, 'dp', [(i, i ^ step) for i in range(size)]))  32.7 us
    unnamed x34, local copies, waits for them, and re-layouts  17.8 us
    dynamic_slice x1, local copies, waits for them, and re-layouts, per_device(): sent = blocks[place ^ step]  10.4 us
    dot_general x1, matrix products, per_device(): shaped = jnp.dot(left, mixed, preferred_element_type=jnp.float32)  9.26 us
    reshape x2, local copies, waits for them, and re-layouts, per_device(): placed.astype(jnp.bfloat16).reshape(row_blocks, block_rows, half_cols)  8.56 us
    all_to_all x1, starting transfers between devices, per_device(): lax.all_to_all(per_owner, 'dp', split_axis=0, concat_axis=0, tiled=True)  8.35 us
    ppermute x15, waiting for transfers between devices, per_device(): outs.append(lax.ppermute(sent, 'dp', [(i, i ^ step) for i in range(size)]))  7.91 us
  transfers between devices with their start and end apart: 16, of which 2 were waited for; matrix products, arithmetic and copies ran while one was open for 21% of the time, Pallas kernels for 0%

profile of v1, /device:TPU:0, one launch (start us, length us, event | category | flops | bytes accessed | tf_op | source)
XLA Modules:
  0.0 180.9 jit_solution(8874958792570150682)
XLA Ops:
  0.0 5.4 %fusion.4 = f32[4,4096]{1,0:T(4,128)S(1)} fusion(f32[4,64,4096]{2,1,0:T(8,128)} %param.6, bf16[4,64,4096]{2,1,0:T(8,128)(2,1)} %param.5), kind=kLoop, calls=%fused_computation.10 | loop fusion | flops 9420800 | bytes 6356992 | tf_op jit(solution)/shard_map/reduce_sum | solution.py:31
  6.5 8.3 %all-to-all-start = ((f32[16,1,1]{2,1,0:T(1,128)}), f32[16,1,1]{2,1,0:T(1,128)S(1)}, u32[]{:S(2)}, u32[]{:S(2)}) async-start(f32[16,1,1]{2,1,0:T(1,128)} %bitcast.56), calls=%async_computation | async-start | bytes 16384 | tf_op jit(solution)/shard_map/all_to_all | solution.py:43
  14.9 4.5 %reshape.69 = bf16[4,64,4,1024]{3,2,1,0:T(4,128)(2,1)} reshape(bf16[4,64,4096]{2,1,0:T(8,128)(2,1)} %param.5) | data formatting | bytes 4194304 | tf_op jit(solution)/shard_map/reshape | solution.py:39
  19.4 4.6 %bitcast_convert_fusion = bf16[16,64,1024]{2,0,1:T(8,128)(2,1)} fusion(bf16[4,64,4,1024]{3,2,1,0:T(4,128)(2,1)} %reshape.69, s32[4,4]{1,0:T(4,128)S(1)} %fusion.27), kind=kOutput, calls=%fused_computation.7 | convolution fusion | flops 34603264 | bytes 4194368 | tf_op jit(solution)/shard_map/src,rwck->swk/dot_general | solution.py:40
  24.0 10.4 %constant_dynamic-slice_fusion = (bf16[1,64,1024]{2,0,1:T(2,128)(2,1)S(1)}, bf16[1,64,1024]{2,0,1:T(2,128)(2,1)S(1)}, bf16[1,64,1024]{2,0,1:T(2,128)(2,1)S(1)}, ...) fusion(bf16[16,64,1024]{2,0,1:T(8,128)(2,1)} %bitcast_convert_f, ...), kind=kLoop, calls=%fused_computation.55 | loop fusion | bytes 4194368 | tf_op jit(solution)/shard_map/dynamic_slice | solution.py:51
  35.1 1.8 %collective-permute-start = (bf16[1,1,64,1024]{3,2,1,0:T(8,128)(2,1)}, bf16[1,1,64,1024]{3,2,1,0:T(8,128)(2,1)}, u32[]{:S(2)}, u32[]{:S(2)}) collective-permute-start(bf16[1,1,64,1024]{3,2,1,0:T(8,128)(2,1)} %bitcast.135), channel_id=1, source_target_pairs={{0,2},{2,0},{4,6},{6,4},{8,10},{10,8},{12,14},{14,12},{16,18},{18,... | collective-permute-start | bytes 393224 | tf_op jit(solution)/shard_map/ppermute | solution.py:52
  40.0 1.9 %collective-permute-start.3 = (bf16[1,1,64,1024]{3,2,1,0:T(8,128)(2,1)S(1)}, bf16[1,1,64,1024]{3,2,1,0:T(8,128)(2,1)}, u32[]{:S(2)}, u32[]{:S(2)}) collective-permute-start(bf16[1,1,64,1024]{3,2,1,0:T(8,128)(2,1)S(1)} %bitcast.149), channel_id=1, source_target_pairs={{0,8},{2,10},{4,12},{6,14},{8,0},{10,2},{12,4},{14,6},{16,24},{18,... | collective-permute-start | bytes 393224 | tf_op jit(solution)/shard_map/ppermute | solution.py:52
  46.8 2.4 %collective-permute-start.5 = (bf16[1,1,64,1024]{3,2,1,0:T(8,128)(2,1)}, bf16[1,1,64,1024]{3,2,1,0:T(8,128)(2,1)S(1)}, u32[]{:S(2)}, u32[]{:S(2)}) collective-permute-start(bf16[1,1,64,1024]{3,2,1,0:T(8,128)(2,1)} %bitcast.150), channel_id=1, source_target_pairs={{0,12},{2,14},{4,8},{6,10},{8,4},{10,6},{12,0},{14,2},{16,28},{18,... | collective-permute-start | bytes 393224 | tf_op jit(solution)/shard_map/ppermute | solution.py:52
  49.2 1.6 bitcast_dynamic-update-slice_fusion.15
  50.9 1.6 bitcast_dynamic-update-slice_fusion.14
  52.5 2.8 %collective-permute-start.7 = (bf16[1,1,64,1024]{3,2,1,0:T(8,128)(2,1)S(1)}, bf16[1,1,64,1024]{3,2,1,0:T(8,128)(2,1)S(1)}, u32[]{:S(2)}, u32[]{:S(2)}) collective-permute-start(bf16[1,1,64,1024]{3,2,1,0:T(8,128)(2,1)S(1)} %bitcast.146), channel_id=1, source_target_pairs={{0,16},{2,18},{4,20},{6,22},{8,24},{10,26},{12,28},{14,30},{16,0},... | collective-permute-start | bytes 393224 | tf_op jit(solution)/shard_map/ppermute | solution.py:52
  55.3 1.6 bitcast_dynamic-update-slice_fusion.13
  59.9 3.3 %collective-permute-start.9 = (bf16[1,1,64,1024]{3,2,1,0:T(8,128)(2,1)S(1)}, bf16[1,1,64,1024]{3,2,1,0:T(8,128)(2,1)S(1)}, u32[]{:S(2)}, u32[]{:S(2)}) collective-permute-start(bf16[1,1,64,1024]{3,2,1,0:T(8,128)(2,1)S(1)} %bitcast.144), channel_id=1, source_target_pairs={{0,20},{2,22},{4,16},{6,18},{8,28},{10,30},{12,24},{14,26},{16,4},... | collective-permute-start | bytes 393224 | tf_op jit(solution)/shard_map/ppermute | solution.py:52
  65.5 3.7 %collective-permute-start.11 = (bf16[1,1,64,1024]{3,2,1,0:T(8,128)(2,1)S(1)}, bf16[1,1,64,1024]{3,2,1,0:T(8,128)(2,1)S(1)}, u32[]{:S(2)}, u32[]{:S(2)}) collective-permute-start(bf16[1,1,64,1024]{3,2,1,0:T(8,128)(2,1)S(1)} %bitcast.142), channel_id=1, source_target_pairs={{0,24},{2,26},{4,28},{6,30},{8,16},{10,18},{12,20},{14,22},{16,8},... | collective-permute-start | bytes 393224 | tf_op jit(solution)/shard_map/ppermute | solution.py:52
  69.9 7.5 %collective-permute-start.12 = (bf16[1,1,64,1024]{3,2,1,0:T(8,128)(2,1)S(1)}, bf16[1,1,64,1024]{3,2,1,0:T(8,128)(2,1)S(1)}, u32[]{:S(2)}, u32[]{:S(2)}) collective-permute-start(bf16[1,1,64,1024]{3,2,1,0:T(8,128)(2,1)S(1)} %bitcast.141), channel_id=1, source_target_pairs={{0,26},{2,24},{4,30},{6,28},{8,18},{10,16},{12,22},{14,20},{16,10}... | collective-permute-start | bytes 393224 | tf_op jit(solution)/shard_map/ppermute | solution.py:52
  78.0 3.0 %collective-permute-start.13 = (bf16[1,1,64,1024]{3,2,1,0:T(8,128)(2,1)S(1)}, bf16[1,1,64,1024]{3,2,1,0:T(8,128)(2,1)S(1)}, u32[]{:S(2)}, u32[]{:S(2)}) collective-permute-start(bf16[1,1,64,1024]{3,2,1,0:T(8,128)(2,1)S(1)} %bitcast.140), channel_id=1, source_target_pairs={{0,28},{2,30},{4,24},{6,26},{8,20},{10,22},{12,16},{14,18},{16,12}... | collective-permute-start | bytes 393224 | tf_op jit(solution)/shard_map/ppermute | solution.py:52
  84.6 7.0 %collective-permute-done.10 = bf16[1,1,64,1024]{3,2,1,0:T(8,128)(2,1)S(1)} collective-permute-done((bf16[1,1,64,1024]{3,2,1,0:T(8,128)(2,1)S(1)}, bf16[1,1,64,1024]{3,2,1,0:T(8,128)(2,1)S(1)}, u32[]{:S(2)}, u32[]{:S(2)}) %collective-permute-start.10) | collective-permute-done | bytes 131104 | tf_op jit(solution)/shard_map/ppermute | solution.py:52
  94.9 3.6 %gather_fusion = bf16[16,64,1024]{2,1,0:T(8,128)(2,1)} fusion(bf16[16,64,1024]{2,1,0:T(8,128)(2,1)} %bitcast.137, s32[1024]{0:T(1024)S(1)} %pad_clamp_fusion), kind=kCustom, calls=%fused_computation | custom fusion | bytes 4194368 | tf_op jit(solution)/shard_map/gather | solution.py:53
  98.5 9.3 %multiply_reduce_fusion = (f32[]{:T(128)}, f32[1024,1024]{0,1:T(8,128)}) fusion(bf16[1024,1024]{1,0:T(8,128)(2,1)} %bitcast.138, bf16[1,1,1024,1024]{3,2,1,0:T(8,128)(2,1)S(1)} %copy-done, bf16[1,1,1024,1024]{3,2,1,0:T(8,128)(2,1)} %param.7), kind=kOutput, calls=%fused_computation.9 | convolution fusion | flops 4298113024 | bytes 10485764 | tf_op jit(solution)/shard_map/dot_general | solution.py:57
  108.5 2.8 %multiply_convert_fusion = bf16[1024,1024]{0,1:T(8,128)(2,1)S(1)} fusion(f32[1024,1024]{0,1:T(8,128)} %get-tuple-element.22, f32[]{:T(128)S(6)} %sqrt.7), kind=kLoop, calls=%fused_computation.8 | loop fusion | flops 2097152 | bytes 6291460 | tf_op jit(solution)/shard_map/convert_element_type | solution.py:60
  111.3 57.9 %all_to_all.18 = bf16[1,16,64,1024]{3,2,0,1:T(8,128)(2,1)S(1)} all-to-all(bf16[1,16,64,1024]{3,2,0,1:T(8,128)(2,1)S(1)} %bitcast.136), channel_id=1, replica_groups=mesh['dp'=16,'mp'=2] {'dp'}, dimensions={1} | all-to-all | bytes 4194304 | tf_op jit(solution)/shard_map/all_to_all | solution.py:61
  169.2 3.1 %convert_bitcast_fusion = bf16[4,64,4,1024]{3,2,0,1:T(4,128)(2,1)} fusion(bf16[1,16,64,1024]{3,2,0,1:T(8,128)(2,1)S(1)} %all_to_all.18, s32[4,4]{1,0:T(4,128)S(1)} %fusion.27), kind=kOutput, calls=%fused_computation.18 | convolution fusion | flops 34603264 | bytes 4194368 | tf_op jit(solution)/shard_map/src,swk->rwck/dot_general | solution.py:62
  172.3 4.5 %reshape.72 = bf16[4,64,4096]{2,0,1:T(4,128)(2,1)} reshape(bf16[4,64,4,1024]{3,2,0,1:T(4,128)(2,1)} %convert_bitcast_fusion) | data formatting | bytes 4194304 | tf_op jit(solution)/shard_map/reshape | solution.py:68
  176.8 4.1 %copy.23 = bf16[4,64,4096]{2,1,0:T(8,128)(2,1)} copy(bf16[4,64,4096]{2,0,1:T(4,128)(2,1)} %reshape.72) | data formatting | bytes 4194304 | tf_op jit(solution)/shard_map/reshape | solution.py:68
  (61 shorter events, 22.8 us)
Async XLA Ops:
  0.0 98.5 %copy-start = (bf16[1,1,1024,1024]{3,2,1,0:T(8,128)(2,1)S(1)}, bf16[1,1,1024,1024]{3,2,1,0:T(8,128)(2,1)}, u32[]{:S(2)}) copy-start(bf16[1,1,1024,1024]{3,2,1,0:T(8,128)(2,1)} %param.8) | copy-start | bytes 6291460
  0.0 5.5 %copy-start.1 = (s32[2,4,4]{2,1,0:T(4,128)S(1)}, s32[2,4,4]{2,1,0:T(4,128)}, u32[]{:S(2)}) copy-start(s32[2,4,4]{2,1,0:T(4,128)} %param.9) | copy-start | bytes 388
  6.5 38.9 %all-to-all-start = ((f32[16,1,1]{2,1,0:T(1,128)}), f32[16,1,1]{2,1,0:T(1,128)S(1)}, u32[]{:S(2)}, u32[]{:S(2)}) async-start(f32[16,1,1]{2,1,0:T(1,128)} %bitcast.56), calls=%async_computation | async-start | bytes 16384 | tf_op jit(solution)/shard_map/all_to_all | solution.py:43
  35.1 11.7 %collective-permute-start = (bf16[1,1,64,1024]{3,2,1,0:T(8,128)(2,1)}, bf16[1,1,64,1024]{3,2,1,0:T(8,128)(2,1)}, u32[]{:S(2)}, u32[]{:S(2)}) collective-permute-start(bf16[1,1,64,1024]{3,2,1,0:T(8,128)(2,1)} %bitcast.135), channel_id=1, source_target_pairs={{0,2},{2,0},{4,6},{6,4},{8,10},{10,8},{12,14},{14,12},{16,18},{18,... | collective-permute-start | bytes 393224 | tf_op jit(solution)/shard_map/ppermute | solution.py:52
  37.6 13.1 %collective-permute-start.1 = (bf16[1,1,64,1024]{3,2,1,0:T(8,128)(2,1)}, bf16[1,1,64,1024]{3,2,1,0:T(8,128)(2,1)}, u32[]{:S(2)}, u32[]{:S(2)}) collective-permute-start(bf16[1,1,64,1024]{3,2,1,0:T(8,128)(2,1)} %bitcast.134), channel_id=1, source_target_pairs={{0,4},{2,6},{4,0},{6,2},{8,12},{10,14},{12,8},{14,10},{16,20},{18,... | collective-permute-start | bytes 393224 | tf_op jit(solution)/shard_map/ppermute | solution.py:52
  39.8 12.7 %collective-permute-start.2 = (bf16[1,1,64,1024]{3,2,1,0:T(8,128)(2,1)}, bf16[1,1,64,1024]{3,2,1,0:T(8,128)(2,1)}, u32[]{:S(2)}, u32[]{:S(2)}) collective-permute-start(bf16[1,1,64,1024]{3,2,1,0:T(8,128)(2,1)} %bitcast.133), channel_id=1, source_target_pairs={{0,6},{2,4},{4,2},{6,0},{8,14},{10,12},{12,10},{14,8},{16,22},{18,... | collective-permute-start | bytes 393224 | tf_op jit(solution)/shard_map/ppermute | solution.py:52
  40.0 16.8 %collective-permute-start.3 = (bf16[1,1,64,1024]{3,2,1,0:T(8,128)(2,1)S(1)}, bf16[1,1,64,1024]{3,2,1,0:T(8,128)(2,1)}, u32[]{:S(2)}, u32[]{:S(2)}) collective-permute-start(bf16[1,1,64,1024]{3,2,1,0:T(8,128)(2,1)S(1)} %bitcast.149), channel_id=1, source_target_pairs={{0,8},{2,10},{4,12},{6,14},{8,0},{10,2},{12,4},{14,6},{16,24},{18,... | collective-permute-start | bytes 393224 | tf_op jit(solution)/shard_map/ppermute | solution.py:52
  42.0 17.9 %collective-permute-start.4 = (bf16[1,1,64,1024]{3,2,1,0:T(8,128)(2,1)S(1)}, bf16[1,1,64,1024]{3,2,1,0:T(8,128)(2,1)}, u32[]{:S(2)}, u32[]{:S(2)}) collective-permute-start(bf16[1,1,64,1024]{3,2,1,0:T(8,128)(2,1)S(1)} %bitcast.147), channel_id=1, source_target_pairs={{0,10},{2,8},{4,14},{6,12},{8,2},{10,0},{12,6},{14,4},{16,26},{18,... | collective-permute-start | bytes 393224 | tf_op jit(solution)/shard_map/ppermute | solution.py:52
  46.8 17.9 %collective-permute-start.5 = (bf16[1,1,64,1024]{3,2,1,0:T(8,128)(2,1)}, bf16[1,1,64,1024]{3,2,1,0:T(8,128)(2,1)S(1)}, u32[]{:S(2)}, u32[]{:S(2)}) collective-permute-start(bf16[1,1,64,1024]{3,2,1,0:T(8,128)(2,1)} %bitcast.150), channel_id=1, source_target_pairs={{0,12},{2,14},{4,8},{6,10},{8,4},{10,6},{12,0},{14,2},{16,28},{18,... | collective-permute-start | bytes 393224 | tf_op jit(solution)/shard_map/ppermute | solution.py:52
  50.8 14.8 %collective-permute-start.6 = (bf16[1,1,64,1024]{3,2,1,0:T(8,128)(2,1)S(1)}, bf16[1,1,64,1024]{3,2,1,0:T(8,128)(2,1)S(1)}, u32[]{:S(2)}, u32[]{:S(2)}) collective-permute-start(bf16[1,1,64,1024]{3,2,1,0:T(8,128)(2,1)S(1)} %bitcast.148), channel_id=1, source_target_pairs={{0,14},{2,12},{4,10},{6,8},{8,6},{10,4},{12,2},{14,0},{16,30},{18,... | collective-permute-start | bytes 393224 | tf_op jit(solution)/shard_map/ppermute | solution.py:52
  52.5 17.4 %collective-permute-start.7 = (bf16[1,1,64,1024]{3,2,1,0:T(8,128)(2,1)S(1)}, bf16[1,1,64,1024]{3,2,1,0:T(8,128)(2,1)S(1)}, u32[]{:S(2)}, u32[]{:S(2)}) collective-permute-start(bf16[1,1,64,1024]{3,2,1,0:T(8,128)(2,1)S(1)} %bitcast.146), channel_id=1, source_target_pairs={{0,16},{2,18},{4,20},{6,22},{8,24},{10,26},{12,28},{14,30},{16,0},... | collective-permute-start | bytes 393224 | tf_op jit(solution)/shard_map/ppermute | solution.py:52
  56.8 21.2 %collective-permute-start.8 = (bf16[1,1,64,1024]{3,2,1,0:T(8,128)(2,1)S(1)}, bf16[1,1,64,1024]{3,2,1,0:T(8,128)(2,1)S(1)}, u32[]{:S(2)}, u32[]{:S(2)}) collective-permute-start(bf16[1,1,64,1024]{3,2,1,0:T(8,128)(2,1)S(1)} %bitcast.145), channel_id=1, source_target_pairs={{0,18},{2,16},{4,22},{6,20},{8,26},{10,24},{12,30},{14,28},{16,2},... | collective-permute-start | bytes 393224 | tf_op jit(solution)/shard_map/ppermute | solution.py:52
  59.9 22.8 %collective-permute-start.9 = (bf16[1,1,64,1024]{3,2,1,0:T(8,128)(2,1)S(1)}, bf16[1,1,64,1024]{3,2,1,0:T(8,128)(2,1)S(1)}, u32[]{:S(2)}, u32[]{:S(2)}) collective-permute-start(bf16[1,1,64,1024]{3,2,1,0:T(8,128)(2,1)S(1)} %bitcast.144), channel_id=1, source_target_pairs={{0,20},{2,22},{4,16},{6,18},{8,28},{10,30},{12,24},{14,26},{16,4},... | collective-permute-start | bytes 393224 | tf_op jit(solution)/shard_map/ppermute | solution.py:52
  64.7 26.9 %collective-permute-start.10 = (bf16[1,1,64,1024]{3,2,1,0:T(8,128)(2,1)S(1)}, bf16[1,1,64,1024]{3,2,1,0:T(8,128)(2,1)S(1)}, u32[]{:S(2)}, u32[]{:S(2)}) collective-permute-start(bf16[1,1,64,1024]{3,2,1,0:T(8,128)(2,1)S(1)} %bitcast.143), channel_id=1, source_target_pairs={{0,22},{2,20},{4,18},{6,16},{8,30},{10,28},{12,26},{14,24},{16,6},... | collective-permute-start | bytes 393224 | tf_op jit(solution)/shard_map/ppermute | solution.py:52
  65.5 26.7 %collective-permute-start.11 = (bf16[1,1,64,1024]{3,2,1,0:T(8,128)(2,1)S(1)}, bf16[1,1,64,1024]{3,2,1,0:T(8,128)(2,1)S(1)}, u32[]{:S(2)}, u32[]{:S(2)}) collective-permute-start(bf16[1,1,64,1024]{3,2,1,0:T(8,128)(2,1)S(1)} %bitcast.142), channel_id=1, source_target_pairs={{0,24},{2,26},{4,28},{6,30},{8,16},{10,18},{12,20},{14,22},{16,8},... | collective-permute-start | bytes 393224 | tf_op jit(solution)/shard_map/ppermute | solution.py:52
  69.9 23.1 %collective-permute-start.12 = (bf16[1,1,64,1024]{3,2,1,0:T(8,128)(2,1)S(1)}, bf16[1,1,64,1024]{3,2,1,0:T(8,128)(2,1)S(1)}, u32[]{:S(2)}, u32[]{:S(2)}) collective-permute-start(bf16[1,1,64,1024]{3,2,1,0:T(8,128)(2,1)S(1)} %bitcast.141), channel_id=1, source_target_pairs={{0,26},{2,24},{4,30},{6,28},{8,18},{10,16},{12,22},{14,20},{16,10}... | collective-permute-start | bytes 393224 | tf_op jit(solution)/shard_map/ppermute | solution.py:52
  78.0 15.6 %collective-permute-start.13 = (bf16[1,1,64,1024]{3,2,1,0:T(8,128)(2,1)S(1)}, bf16[1,1,64,1024]{3,2,1,0:T(8,128)(2,1)S(1)}, u32[]{:S(2)}, u32[]{:S(2)}) collective-permute-start(bf16[1,1,64,1024]{3,2,1,0:T(8,128)(2,1)S(1)} %bitcast.140), channel_id=1, source_target_pairs={{0,28},{2,30},{4,24},{6,26},{8,20},{10,22},{12,16},{14,18},{16,12}... | collective-permute-start | bytes 393224 | tf_op jit(solution)/shard_map/ppermute | solution.py:52
  82.6 11.6 %collective-permute-start.14 = (bf16[1,1,64,1024]{3,2,1,0:T(8,128)(2,1)S(1)}, bf16[1,1,64,1024]{3,2,1,0:T(8,128)(2,1)S(1)}, u32[]{:S(2)}, u32[]{:S(2)}) collective-permute-start(bf16[1,1,64,1024]{3,2,1,0:T(8,128)(2,1)S(1)} %bitcast.139), channel_id=1, source_target_pairs={{0,30},{2,28},{4,26},{6,24},{8,22},{10,20},{12,18},{14,16},{16,14}... | collective-permute-start | bytes 393224 | tf_op jit(solution)/shard_map/ppermute | solution.py:52
